TPU v7x, 256 devices: a whole 4x4x8 slice. The times are simulated.
256 devices in a mesh: rows: 64 (over x, y, z_lo), rep: 4 (over z_hi, core).
Axes of the slice: x: 4, y: 4, z: 8 (z_hi: 2, z_lo: 4; z = z_hi * 4 + z_lo), core: 2. Of those that a mesh axis runs over, the one named last changes fastest.
Arguments:
- x_tiles: bfloat16 [512, 10, 128, 128], P('rows'), may hold values from -2.5 to 2.5
- giant_tiles: bfloat16 [512, 10, 128, 128], P('rows'), may hold values from -2.5 to 2.5
- coeffs: float32 [3], replicated, may hold values from 0.5 to 1.5
- pattern: int32 [512, 10], replicated, may hold values from 0 to 511, as said below
Outputs:
- squared: bfloat16 [512, 10, 128, 128], P('rows')
- result: bfloat16 [512, 10, 128, 128], P('rows')
Inputs may be any that keep to these rules, and one draw needn't show every extreme that they name: `pattern`: slots 2 j and 2 j + 1 of block row i hold two different tile columns of panel (i // 8 + j - 2) mod (64), a panel being 8 consecutive block rows, for j = 0 to 4; slot 4 holds i itself.
All inputs are finite; a program needn't handle non-finite values.
Results may differ from a plain program's by a relative error of at most 0.012.
Values may be sent and summed in bfloat16 or wider, within the bound.
A program may use at most 128 MiB of HBM per device.

v0:
```python
import jax
import jax.numpy as jnp
from jax import lax
from jax.sharding import PartitionSpec as P

HALF = 2
KP = 2


def passed_along(block, axis, distance):
    devices = range(lax.axis_size(axis))
    route = [((i - distance) % len(devices), i) for i in devices]
    return lax.ppermute(block, axis, route)


def panel_terms(left_tiles, left_cols, slot_start, panel_tiles, pattern, base_row):
    tile_count = left_cols.shape[1]
    left_part = lax.dynamic_slice_in_dim(left_tiles, slot_start, KP, 1)
    cols_part = lax.dynamic_slice_in_dim(left_cols, slot_start, KP, 1)
    local_rows = cols_part - base_row
    right_cols = jnp.take(pattern, cols_part, axis=0)
    matches = right_cols[:, :, :, None] == left_cols[:, None, None, :]
    places = jnp.arange(tile_count, dtype=jnp.int32)[None, None, :, None]
    slot_pick = jnp.sum(jnp.where(matches, places, 0), axis=2)
    slot_found = jnp.any(matches, axis=2)
    flat_tiles = panel_tiles.reshape((-1,) + panel_tiles.shape[2:])
    chosen = jnp.take(flat_tiles, local_rows[:, :, None] * tile_count + slot_pick, axis=0)
    chosen = jnp.where(slot_found[:, :, :, None, None], chosen, jnp.zeros((), chosen.dtype))
    return jnp.einsum("raxz,rauzy->ruxy", left_part, chosen, preferred_element_type=jnp.float32)


def local(x_tiles, giant_tiles, coeffs, pattern):
    blocks = x_tiles.shape[0]
    panels = lax.axis_size("rows")
    device = lax.axis_index("rows")
    my_cols = lax.dynamic_slice_in_dim(pattern, device * blocks, blocks, 0)
    tile_count = pattern.shape[1]
    diagonal_slot = (jnp.arange(tile_count, dtype=jnp.int32) == HALF * KP).astype(jnp.float32)
    identity = (
        diagonal_slot[:, None, None] * jnp.eye(x_tiles.shape[2], dtype=jnp.float32)[None, :, :]
    )

    def base_of(offset):
        return (device + offset) % panels * blocks

    def every_product(left, right):
        total = panel_terms(left, my_cols, HALF * KP, right, pattern, base_of(0))
        below = right
        above = right
        for step in range(1, HALF + 1):
            below = passed_along(below, "rows", 1)
            above = passed_along(above, "rows", -1)
            total = total + panel_terms(
                left, my_cols, (HALF - step) * KP, below, pattern, base_of(-step)
            )
            total = total + panel_terms(
                left, my_cols, (HALF + step) * KP, above, pattern, base_of(step)
            )
        return total

    squared = every_product(x_tiles, x_tiles).astype(jnp.bfloat16)
    mixed = (
        coeffs[0] * identity[None]
        + coeffs[1] * x_tiles.astype(jnp.float32)
        + coeffs[2] * squared.astype(jnp.float32)
    )
    baby_tiles = mixed.astype(jnp.bfloat16)
    result = every_product(giant_tiles, baby_tiles).astype(jnp.bfloat16)
    return (squared, result)


def solution(mesh):
    return jax.shard_map(
        local,
        mesh=mesh,
        in_specs=(P("rows", None, None, None), P("rows", None, None, None), P(), P()),
        out_specs=(P("rows", None, None, None), P("rows", None, None, None)),
        check_vma=False,
    )
```

profile of v0, /device:TPU:1, one launch (start us, length us, event | category | flops | bytes accessed | tf_op | source)
XLA Modules:
  0.0 509.9 jit_solution(5765595598062591118)
XLA Ops:
  0.6 2.5 collective-permute-start
  3.2 7.4 %collective-permute-start.1 = (bf16[8,10,128,128]{3,2,1,0:T(8,128)(2,1)}, bf16[8,10,128,128]{3,2,1,0:T(8,128)(2,1)}, u32[]{:S(2)}, u32[]{:S(2)}) collective-permute-start(bf16[8,10,128,128]{3,2,1,0:T(8,128)(2,1)} %param.8), channel_id=1, source_target_pairs={{4,0},{8,4},{12,8},{16,12},{20,16},{24,20},{28,24},{32,28},{36,32}... | collective-permute-start | bytes 7864328 | tf_op jit(solution)/shard_map/ppermute | solution.py:13
  10.6 0.9 copy.105
  11.5 0.9 compare_and_fusion.9
  12.6 0.1 copy.103
  12.7 0.6 gather_fusion
  13.4 0.1 copy.106
  13.6 0.6 gather_fusion.2
  14.2 0.1 copy.112
  14.4 0.1 copy.115
  14.6 0.6 gather_fusion.4
  15.2 0.1 copy.120
  15.4 0.1 copy.123
  15.7 0.6 gather_fusion.6
  16.2 0.1 copy.128
  16.4 0.1 copy.131
  16.7 0.6 gather_fusion.8
  17.2 0.1 copy.136
  17.4 0.1 copy.139
  17.5 0.8 constant_dynamic-slice_fusion
  18.4 0.9 subtract_multiply_fusion
  19.3 0.2 fusion.78
  20.2 0.2 compare_reduce_fusion
  20.4 46.6 %collective-permute-done = bf16[8,10,128,128]{3,2,1,0:T(8,128)(2,1)} collective-permute-done((bf16[8,10,128,128]{3,2,1,0:T(8,128)(2,1)}, bf16[8,10,128,128]{3,2,1,0:T(8,128)(2,1)}, u32[]{:S(2)}, u32[]{:S(2)}) %collective-permute-start) | collective-permute-done | bytes 2621472 | tf_op jit(solution)/shard_map/ppermute | solution.py:13
  67.0 50.6 %collective-permute-done.1 = bf16[8,10,128,128]{3,2,1,0:T(8,128)(2,1)} collective-permute-done((bf16[8,10,128,128]{3,2,1,0:T(8,128)(2,1)}, bf16[8,10,128,128]{3,2,1,0:T(8,128)(2,1)}, u32[]{:S(2)}, u32[]{:S(2)}) %collective-permute-start.1) | collective-permute-done | bytes 2621472 | tf_op jit(solution)/shard_map/ppermute | solution.py:13
  117.6 6.1 %collective-permute-start.3 = (bf16[8,10,128,128]{3,2,1,0:T(8,128)(2,1)}, bf16[8,10,128,128]{3,2,1,0:T(8,128)(2,1)}, u32[]{:S(2)}, u32[]{:S(2)}) collective-permute-start(bf16[8,10,128,128]{3,2,1,0:T(8,128)(2,1)} %collective-permute-done.1), channel_id=1, source_target_pairs={{4,0},{8,4},{12,8},{16,12},{20,16},{24,20},{28,24},{32,28},{36,32}... | collective-permute-start | bytes 7864328 | tf_op jit(solution)/shard_map/ppermute | solution.py:13
  123.8 4.4 copy.145
  128.4 7.7 %gather_fusion.1 = bf16[160,128,128]{2,1,0:T(8,128)(2,1)} fusion(bf16[80,128,128]{2,1,0:T(8,128)(2,1)S(1)} %bitcast.194, s32[1024]{0:T(1024)S(1)} %pad_clamp_fusion.8), kind=kCustom, calls=%fused_computation.1.clone | custom fusion | bytes 10486400 | tf_op jit(solution)/shard_map/jit(_take)/gather | solution.py:27
  136.2 0.6 fusion.100
  136.8 0.8 multiply_multiply_fusion
  137.6 7.0 %fusion.11 = f32[8,10,128,128,1]{3,2,1,4,0:T(8,128)} fusion(bf16[8,2,10,128,128]{4,3,2,1,0:T(8,128)(2,1)} %bitcast.197, pred[8,2,10]{2,1,0:T(4,128)(4,1)S(1)} %copy.109, pred[8,2,10]{2,1,0:T(4,128)(4,1)S(1)} %copy.108, bf16[8,10,128,128]{3,2,1,0:T(8,128)(2,1)S(1)} %copy-done), kind=kOutput, calls=%fused_computation.44 | convolution fusion | flops 676331520 | bytes 11018240 | tf_op jit(solution)/shard_map/raxz,rauzy->ruxy/dot_general | solution.py:29
  144.5 9.4 %gather_fusion.3 = bf16[160,128,128]{2,1,0:T(8,128)(2,1)} fusion(bf16[80,128,128]{2,1,0:T(8,128)(2,1)} %bitcast.8, s32[1024]{0:T(1024)S(1)} %pad_clamp_fusion.6), kind=kCustom, calls=%fused_computation.6.clone | custom fusion | bytes 10486400 | tf_op jit(solution)/shard_map/jit(_take)/gather | solution.py:27
  153.9 10.0 %gather_fusion.5 = bf16[160,128,128]{2,1,0:T(8,128)(2,1)} fusion(bf16[80,128,128]{2,1,0:T(8,128)(2,1)} %bitcast.15, s32[1024]{0:T(1024)S(1)} %pad_clamp_fusion.4), kind=kCustom, calls=%fused_computation.7.clone | custom fusion | bytes 10486400 | tf_op jit(solution)/shard_map/jit(_take)/gather | solution.py:27
  163.9 7.2 %fusion.10 = f32[8,10,128,128,1]{3,2,1,4,0:T(8,128)} fusion(bf16[8,2,10,128,128]{4,3,2,1,0:T(8,128)(2,1)} %bitcast.203, pred[8,2,10]{2,1,0:T(4,128)(4,1)S(1)} %copy.117, pred[8,2,10]{2,1,0:T(4,128)(4,1)S(1)} %copy.116, bf16[8,10,128,128]{3,2,1,0:T(8,128)(2,1)S(1)} %copy-done), kind=kOutput, calls=%fused_computation.42 | convolution fusion | flops 676331520 | bytes 11018240 | tf_op jit(solution)/shard_map/raxz,rauzy->ruxy/dot_general | solution.py:29
  171.1 4.1 fusion.9
  175.2 1.2 collective-permute-done.2
  176.4 9.5 %gather_fusion.7 = bf16[160,128,128]{2,1,0:T(8,128)(2,1)} fusion(bf16[80,128,128]{2,1,0:T(8,128)(2,1)} %bitcast.22, s32[1024]{0:T(1024)S(1)} %pad_clamp_fusion.2), kind=kCustom, calls=%fused_computation.8.clone | custom fusion | bytes 10486400 | tf_op jit(solution)/shard_map/jit(_take)/gather | solution.py:27
  185.8 46.3 %collective-permute-done.3 = bf16[8,10,128,128]{3,2,1,0:T(8,128)(2,1)} collective-permute-done((bf16[8,10,128,128]{3,2,1,0:T(8,128)(2,1)}, bf16[8,10,128,128]{3,2,1,0:T(8,128)(2,1)}, u32[]{:S(2)}, u32[]{:S(2)}) %collective-permute-start.3) | collective-permute-done | bytes 2621472 | tf_op jit(solution)/shard_map/ppermute | solution.py:13
  232.1 9.5 %gather_fusion.9 = bf16[160,128,128]{2,1,0:T(8,128)(2,1)} fusion(bf16[80,128,128]{2,1,0:T(8,128)(2,1)} %bitcast.29, s32[1024]{0:T(1024)S(1)} %pad_clamp_fusion), kind=kCustom, calls=%fused_computation.9.clone | custom fusion | bytes 10486400 | tf_op jit(solution)/shard_map/jit(_take)/gather | solution.py:27
  241.6 7.0 %fusion.8 = f32[8,10,128,128,1]{3,2,1,4,0:T(8,128)} fusion(bf16[8,2,10,128,128]{4,3,2,1,0:T(8,128)(2,1)} %bitcast.200, pred[8,2,10]{2,1,0:T(4,128)(4,1)S(1)} %copy.133, pred[8,2,10]{2,1,0:T(4,128)(4,1)S(1)} %copy.132, bf16[8,10,128,128]{3,2,1,0:T(8,128)(2,1)S(1)} %copy-done), kind=kOutput, calls=%fused_computation.38 | convolution fusion | flops 676331520 | bytes 11018240 | tf_op jit(solution)/shard_map/raxz,rauzy->ruxy/dot_general | solution.py:29
  248.7 11.9 %add_convert_fusion = (bf16[8,10,128,128]{2,3,1,0:T(8,128)(2,1)}, bf16[8,10,128,128]{2,3,1,0:T(8,128)(2,1)}) fusion(bf16[8,10,128,128]{2,3,1,0:T(8,128)(2,1)S(1)} %copy-done.1, f32[]{:T(128)} %bitcast.38, f32[]{:T(128)} %bitcast.37, f32[10,128,128]{1,2,0:T(8,128)S(1)} %multiply_multiply_fusion, bf16[8,10,128,128]{3,2,1,0:T(8,128)(2,1)S(1)} %copy-done, ...), kind=kOutput, calls=%fused_computation.45 | convolution fusion | flops 692060160 | bytes 35266568 | tf_op jit(solution)/shard_map/raxz,rauzy->ruxy/dot_general | solution.py:29
  260.7 0.3 collective-permute-start.4
  260.9 7.2 %collective-permute-start.5 = (bf16[8,10,128,128]{2,3,1,0:T(8,128)(2,1)}, bf16[8,10,128,128]{2,3,1,0:T(8,128)(2,1)}, u32[]{:S(2)}, u32[]{:S(2)}) collective-permute-start(bf16[8,10,128,128]{2,3,1,0:T(8,128)(2,1)} %get-tuple-element.58), channel_id=1, source_target_pairs={{4,0},{8,4},{12,8},{16,12},{20,16},{24,20},{28,24},{32,28},{36,32}... | collective-permute-start | bytes 7864328 | tf_op jit(solution)/shard_map/ppermute | solution.py:13
  268.1 49.1 %collective-permute-done.4 = bf16[8,10,128,128]{2,3,1,0:T(8,128)(2,1)} collective-permute-done((bf16[8,10,128,128]{2,3,1,0:T(8,128)(2,1)}, bf16[8,10,128,128]{2,3,1,0:T(8,128)(2,1)}, u32[]{:S(2)}, u32[]{:S(2)}) %collective-permute-start.4) | collective-permute-done | bytes 2621472 | tf_op jit(solution)/shard_map/ppermute | solution.py:13
  317.3 3.2 copy.147
  320.5 7.7 %gather_fusion.10 = bf16[160,128,128]{2,1,0:T(8,128)(2,1)} fusion(bf16[80,128,128]{2,1,0:T(8,128)(2,1)S(1)} %copy.147, s32[1024]{0:T(1024)S(1)} %pad_clamp_fusion.8), kind=kCustom, calls=%fused_computation.10.clone | custom fusion | bytes 10486400 | tf_op jit(solution)/shard_map/jit(_take)/gather | solution.py:27
  328.3 4.4 copy.165
  332.6 43.1 %collective-permute-done.5 = bf16[8,10,128,128]{2,3,1,0:T(8,128)(2,1)} collective-permute-done((bf16[8,10,128,128]{2,3,1,0:T(8,128)(2,1)}, bf16[8,10,128,128]{2,3,1,0:T(8,128)(2,1)}, u32[]{:S(2)}, u32[]{:S(2)}) %collective-permute-start.5) | collective-permute-done | bytes 2621472 | tf_op jit(solution)/shard_map/ppermute | solution.py:13
  375.7 7.1 %fusion.6 = f32[8,10,128,128,1]{3,2,1,4,0:T(8,128)} fusion(bf16[8,2,10,128,128]{4,3,2,1,0:T(8,128)(2,1)} %bitcast.196, pred[8,2,10]{2,1,0:T(4,128)(4,1)S(1)} %copy.109, pred[8,2,10]{2,1,0:T(4,128)(4,1)S(1)} %copy.108, bf16[8,10,128,128]{3,2,1,0:T(8,128)(2,1)} %param.9), kind=kOutput, calls=%fused_computation.34 | convolution fusion | flops 676331520 | bytes 11010368 | tf_op jit(solution)/shard_map/raxz,rauzy->ruxy/dot_general | solution.py:29
  382.8 3.4 copy.155
  386.2 7.8 %gather_fusion.12 = bf16[160,128,128]{2,1,0:T(8,128)(2,1)} fusion(bf16[80,128,128]{2,1,0:T(8,128)(2,1)S(1)} %copy.155, s32[1024]{0:T(1024)S(1)} %pad_clamp_fusion.4), kind=kCustom, calls=%fused_computation.12.clone | custom fusion | bytes 10486400 | tf_op jit(solution)/shard_map/jit(_take)/gather | solution.py:27
  394.0 3.2 copy.151
  397.2 7.6 %gather_fusion.11 = bf16[160,128,128]{2,1,0:T(8,128)(2,1)} fusion(bf16[80,128,128]{2,1,0:T(8,128)(2,1)S(1)} %copy.151, s32[1024]{0:T(1024)S(1)} %pad_clamp_fusion.6), kind=kCustom, calls=%fused_computation.11.clone | custom fusion | bytes 10486400 | tf_op jit(solution)/shard_map/jit(_take)/gather | solution.py:27
  404.9 7.3 %fusion.4 = f32[8,10,128,128,1]{3,2,1,4,0:T(8,128)} fusion(bf16[8,2,10,128,128]{4,3,2,1,0:T(8,128)(2,1)} %bitcast.198, pred[8,2,10]{2,1,0:T(4,128)(4,1)S(1)} %copy.125, pred[8,2,10]{2,1,0:T(4,128)(4,1)S(1)} %copy.124, bf16[8,10,128,128]{3,2,1,0:T(8,128)(2,1)} %param.9), kind=kOutput, calls=%fused_computation.30 | convolution fusion | flops 676331520 | bytes 11010368 | tf_op jit(solution)/shard_map/raxz,rauzy->ruxy/dot_general | solution.py:29
  412.2 4.9 fusion.5
  417.1 12.6 %collective-permute-done.6 = bf16[8,10,128,128]{2,3,1,0:T(8,128)(2,1)} collective-permute-done((bf16[8,10,128,128]{2,3,1,0:T(8,128)(2,1)}, bf16[8,10,128,128]{2,3,1,0:T(8,128)(2,1)}, u32[]{:S(2)}, u32[]{:S(2)}) %collective-permute-start.6) | collective-permute-done | bytes 2621472 | tf_op jit(solution)/shard_map/ppermute | solution.py:13
  429.7 3.2 copy.159
  432.9 7.9 %gather_fusion.13 = bf16[160,128,128]{2,1,0:T(8,128)(2,1)} fusion(bf16[80,128,128]{2,1,0:T(8,128)(2,1)S(1)} %copy.159, s32[1024]{0:T(1024)S(1)} %pad_clamp_fusion.2), kind=kCustom, calls=%fused_computation.13.clone | custom fusion | bytes 10486400 | tf_op jit(solution)/shard_map/jit(_take)/gather | solution.py:27
  440.9 7.0 %fusion.3 = f32[8,10,128,128,1]{3,2,1,4,0:T(8,128)} fusion(bf16[8,2,10,128,128]{4,3,2,1,0:T(8,128)(2,1)} %bitcast.201, pred[8,2,10]{2,1,0:T(4,128)(4,1)S(1)} %copy.133, pred[8,2,10]{2,1,0:T(4,128)(4,1)S(1)} %copy.132, bf16[8,10,128,128]{3,2,1,0:T(8,128)(2,1)} %param.9), kind=kOutput, calls=%fused_computation.28 | convolution fusion | flops 676331520 | bytes 11010368 | tf_op jit(solution)/shard_map/raxz,rauzy->ruxy/dot_general | solution.py:29
  447.9 38.1 %collective-permute-done.7 = bf16[8,10,128,128]{2,3,1,0:T(8,128)(2,1)} collective-permute-done((bf16[8,10,128,128]{2,3,1,0:T(8,128)(2,1)}, bf16[8,10,128,128]{2,3,1,0:T(8,128)(2,1)}, u32[]{:S(2)}, u32[]{:S(2)}) %collective-permute-start.7) | collective-permute-done | bytes 2621472 | tf_op jit(solution)/shard_map/ppermute | solution.py:13
  486.0 3.2 copy.163
  489.2 7.7 %gather_fusion.14 = bf16[160,128,128]{2,1,0:T(8,128)(2,1)} fusion(bf16[80,128,128]{2,1,0:T(8,128)(2,1)S(1)} %copy.163, s32[1024]{0:T(1024)S(1)} %pad_clamp_fusion), kind=kCustom, calls=%fused_computation.14.clone | custom fusion | bytes 10486400 | tf_op jit(solution)/shard_map/jit(_take)/gather | solution.py:27
  496.9 10.1 %fusion.33 = bf16[8,10,128,128]{2,3,1,0:T(8,128)(2,1)S(1)} fusion(f32[8,10,128,128,1]{3,2,1,4,0:T(8,128)} %fusion.3, f32[8,10,128,128,1]{3,2,1,4,0:T(8,128)} %fusion.4, f32[8,10,128,128,1]{3,2,1,4,0:T(8,128)} %fusion.5, f32[8,10,128,128,1]{3,2,1,4,0:T(8,128)} %fusion.6, bf16[8,2,10,128,128]{4,3,2,1,0:T(8,128)(2,1)} %bitcast.193, ...), kind=kOutput, calls=%fused_computation.67 | convolution fusion | flops 682885120 | bytes 29360448 | tf_op jit(solution)/shard_map/raxz,rauzy->ruxy/dot_general | solution.py:29
  507.1 2.6 copy.166
  (69 shorter events, 2.2 us)
Async XLA Ops:
  0.6 127.8 %copy-start = (bf16[8,10,128,128]{3,2,1,0:T(8,128)(2,1)S(1)}, bf16[8,10,128,128]{3,2,1,0:T(8,128)(2,1)}, u32[]{:S(2)}) copy-start(bf16[8,10,128,128]{3,2,1,0:T(8,128)(2,1)} %param.8) | copy-start | bytes 7864324
  0.6 66.3 %collective-permute-start = (bf16[8,10,128,128]{3,2,1,0:T(8,128)(2,1)}, bf16[8,10,128,128]{3,2,1,0:T(8,128)(2,1)}, u32[]{:S(2)}, u32[]{:S(2)}) collective-permute-start(bf16[8,10,128,128]{3,2,1,0:T(8,128)(2,1)} %param.8), channel_id=1, source_target_pairs={{252,0},{0,4},{4,8},{8,12},{12,16},{16,20},{20,24},{24,28},{28,32}... | collective-permute-start | bytes 7864328 | tf_op jit(solution)/shard_map/ppermute | solution.py:13
  3.2 114.4 %collective-permute-start.1 = (bf16[8,10,128,128]{3,2,1,0:T(8,128)(2,1)}, bf16[8,10,128,128]{3,2,1,0:T(8,128)(2,1)}, u32[]{:S(2)}, u32[]{:S(2)}) collective-permute-start(bf16[8,10,128,128]{3,2,1,0:T(8,128)(2,1)} %param.8), channel_id=1, source_target_pairs={{4,0},{8,4},{12,8},{16,12},{20,16},{24,20},{28,24},{32,28},{36,32}... | collective-permute-start | bytes 7864328 | tf_op jit(solution)/shard_map/ppermute | solution.py:13
  67.0 109.4 %collective-permute-start.2 = (bf16[8,10,128,128]{3,2,1,0:T(8,128)(2,1)}, bf16[8,10,128,128]{3,2,1,0:T(8,128)(2,1)}, u32[]{:S(2)}, u32[]{:S(2)}) collective-permute-start(bf16[8,10,128,128]{3,2,1,0:T(8,128)(2,1)} %collective-permute-done), channel_id=1, source_target_pairs={{252,0},{0,4},{4,8},{8,12},{12,16},{16,20},{20,24},{24,28},{28,32}... | collective-permute-start | bytes 7864328 | tf_op jit(solution)/shard_map/ppermute | solution.py:13
  117.6 114.5 %collective-permute-start.3 = (bf16[8,10,128,128]{3,2,1,0:T(8,128)(2,1)}, bf16[8,10,128,128]{3,2,1,0:T(8,128)(2,1)}, u32[]{:S(2)}, u32[]{:S(2)}) collective-permute-start(bf16[8,10,128,128]{3,2,1,0:T(8,128)(2,1)} %collective-permute-done.1), channel_id=1, source_target_pairs={{4,0},{8,4},{12,8},{16,12},{20,16},{24,20},{28,24},{32,28},{36,32}... | collective-permute-start | bytes 7864328 | tf_op jit(solution)/shard_map/ppermute | solution.py:13
  128.4 7.8 %copy-start.4 = (f32[3]{0:T(128)S(1)}, f32[3]{0:T(128)}, u32[]{:S(2)}) copy-start(f32[3]{0:T(128)} %param.10) | copy-start | bytes 40
  163.9 7.2 %copy-start.3 = (bf16[160,128,128]{2,1,0:T(8,128)(2,1)S(1)}, bf16[160,128,128]{2,1,0:T(8,128)(2,1)}, u32[]{:S(2)}) copy-start(bf16[160,128,128]{2,1,0:T(8,128)(2,1)} %gather_fusion.5) | copy-start | bytes 15728644
  241.6 7.1 %slice-start = ((s8[5242880]{0:T(1024)(128)(4,1)}), s8[4194304]{0:T(1024)(128)(4,1)S(1)}, s32[]{:S(2)}) async-start(s8[5242880]{0:T(1024)(128)(4,1)} %bitcast.190), calls=%async_computation | async-start | bytes 8388608
  241.6 7.1 %slice-start.1 = ((s8[5242880]{0:T(1024)(128)(4,1)}), s8[1048576]{0:T(1024)(128)(4,1)S(1)}, s32[]{:S(2)}) async-start(s8[5242880]{0:T(1024)(128)(4,1)} %bitcast.190), calls=%async_computation.1 | async-start | bytes 2097152
  241.6 7.1 %copy-start.1 = (bf16[8,10,128,128]{2,3,1,0:T(8,128)(2,1)S(1)}, bf16[8,10,128,128]{2,3,1,0:T(8,128)(2,1)}, u32[]{:S(2)}) copy-start(bf16[8,10,128,128]{2,3,1,0:T(8,128)(2,1)} %copy.145) | copy-start | bytes 7864324
  260.7 56.6 %collective-permute-start.4 = (bf16[8,10,128,128]{2,3,1,0:T(8,128)(2,1)}, bf16[8,10,128,128]{2,3,1,0:T(8,128)(2,1)}, u32[]{:S(2)}, u32[]{:S(2)}) collective-permute-start(bf16[8,10,128,128]{2,3,1,0:T(8,128)(2,1)} %get-tuple-element.58), channel_id=1, source_target_pairs={{252,0},{0,4},{4,8},{8,12},{12,16},{16,20},{20,24},{24,28},{28,32}... | collective-permute-start | bytes 7864328 | tf_op jit(solution)/shard_map/ppermute | solution.py:13
  260.9 114.8 %collective-permute-start.5 = (bf16[8,10,128,128]{2,3,1,0:T(8,128)(2,1)}, bf16[8,10,128,128]{2,3,1,0:T(8,128)(2,1)}, u32[]{:S(2)}, u32[]{:S(2)}) collective-permute-start(bf16[8,10,128,128]{2,3,1,0:T(8,128)(2,1)} %get-tuple-element.58), channel_id=1, source_target_pairs={{4,0},{8,4},{12,8},{16,12},{20,16},{24,20},{28,24},{32,28},{36,32}... | collective-permute-start | bytes 7864328 | tf_op jit(solution)/shard_map/ppermute | solution.py:13
  317.3 112.4 %collective-permute-start.6 = (bf16[8,10,128,128]{2,3,1,0:T(8,128)(2,1)}, bf16[8,10,128,128]{2,3,1,0:T(8,128)(2,1)}, u32[]{:S(2)}, u32[]{:S(2)}) collective-permute-start(bf16[8,10,128,128]{2,3,1,0:T(8,128)(2,1)} %collective-permute-done.4), channel_id=1, source_target_pairs={{252,0},{0,4},{4,8},{8,12},{12,16},{16,20},{20,24},{24,28},{28,32}... | collective-permute-start | bytes 7864328 | tf_op jit(solution)/shard_map/ppermute | solution.py:13
  375.7 110.3 %collective-permute-start.7 = (bf16[8,10,128,128]{2,3,1,0:T(8,128)(2,1)}, bf16[8,10,128,128]{2,3,1,0:T(8,128)(2,1)}, u32[]{:S(2)}, u32[]{:S(2)}) collective-permute-start(bf16[8,10,128,128]{2,3,1,0:T(8,128)(2,1)} %collective-permute-done.5), channel_id=1, source_target_pairs={{4,0},{8,4},{12,8},{16,12},{20,16},{24,20},{28,24},{32,28},{36,32}... | collective-permute-start | bytes 7864328 | tf_op jit(solution)/shard_map/ppermute | solution.py:13
  404.9 7.3 %copy-start.2 = (bf16[160,128,128]{2,1,0:T(8,128)(2,1)S(1)}, bf16[160,128,128]{2,1,0:T(8,128)(2,1)}, u32[]{:S(2)}) copy-start(bf16[160,128,128]{2,1,0:T(8,128)(2,1)} %gather_fusion.11) | copy-start | bytes 15728644
where the time goes:
time: 517 us; the launch traced here: 510 us
  waiting for transfers between devices  288 us (56%)
  local copies, waits for them, and re-layouts  120 us (23%)
  matrix products  73.6 us (14%)
  starting transfers between devices  23.6 us (5%)
    ppermute x8, waiting for transfers between devices, passed_along(): return lax.ppermute(block, axis, route)  288 us
    gather x10, local copies, waits for them, and re-layouts, panel_terms(): jnp.take(flat_tiles, local_rows[:, :, None] * tile_count + slot_pick, axi...  84.9 us
    dot_general x10, matrix products, panel_terms(): jnp.einsum('raxz,rauzy->ruxy', left_part, chosen, preferred_element_type=...  73.6 us
    ppermute x8, starting transfers between devices, passed_along(): return lax.ppermute(block, axis, route)  23.6 us
    reshape x5, local copies, waits for them, and re-layouts, panel_terms(): flat_tiles = panel_tiles.reshape((-1,) + panel_tiles.shape[2:])  16.3 us
    unnamed x18, local copies, waits for them, and re-layouts  12.2 us
  transfers between devices with their start and end apart: 8, of which 8 were waited for; matrix products, arithmetic and copies ran while one was open for 28% of the time, Pallas kernels for 0%

commit v1 on v0

v1 whole, which is shorter than its diff:
```python
import functools

import jax
import jax.numpy as jnp
from jax import lax
from jax.experimental import pallas as pl
from jax.experimental.pallas import tpu as pltpu
from jax.sharding import PartitionSpec as P

HALF = 2
KP = 2
SPREAD = 2 * HALF + 1
UNROLL = 4
MESH = pl.DeviceIdType.MESH

ORDER = (
    ((1, 1), (1, 0), (1, -1), (1, 2), (2, 2), (2, 1), (2, 0)),
    ((1, -1), (1, 0), (1, 2), (1, 1), (2, 0), (2, 1), (2, 2)),
)
NEAR = 4
GROUPS = len(ORDER[0])


def kernel(panels, run, copies, pat, coef, x_hbm, g_hbm, squared_hbm, result_hbm, *scratch):
    (xv, gv, bv, sv, rv, acc, near0, near1, far0, far1, load_sem, out_sem, send_sem, recv_sem, push_sem, pull_sem) = _unpack(scratch)
    rows = xv.shape[0]
    side = xv.shape[2]
    half = rows // 2
    panel = lax.axis_index("rows")
    rep = lax.axis_index("rep")
    core = rep % 2
    zone = rep // 2
    place = panel % run
    if copies > 1:
        zone_up = jnp.where(place == run - 1, 1 - zone, zone)
        zone_down = jnp.where(place == 0, 1 - zone, zone)
    else:
        zone_up = zone
        zone_down = zone
    above = ((panel + 1) % panels, zone_up * 2 + core)
    below = ((panel + panels - 1) % panels, zone_down * 2 + core)
    partner = (panel, zone * 2 + 1 - core)

    loads = [pltpu.make_async_copy(x_hbm, xv, load_sem.at[0]), pltpu.make_async_copy(g_hbm, gv, load_sem.at[1])]
    for load in loads:
        load.start()

    barrier = pltpu.get_barrier_semaphore()
    for other in (above, below, partner):
        pl.semaphore_signal(barrier, inc=1, device_id=other, device_id_type=MESH)
    pl.semaphore_wait(barrier, 3)

    near = (near0, near1)
    far = (far0, far1)
    mine = (xv, bv)
    my_half = pl.ds(core * half, half)
    sends = []

    def landing(phase, group):
        return near[phase][group] if group < NEAR else far[phase][group - NEAR]

    def hop(phase, group, end):
        distance, column = ORDER[phase][group]
        sign = 1 - 2 * end
        slots = sign * (column - distance) + HALF
        if distance == 1:
            source = mine[phase].at[my_half, pl.ds(slots * KP, KP)]
        else:
            source = landing(phase, ORDER[phase].index((1, column - 1))).at[end, my_half]
        index = (phase * GROUPS + group) * 2 + end
        return pltpu.make_async_remote_copy(
            src_ref=source,
            dst_ref=landing(phase, group).at[end, my_half],
            send_sem=send_sem.at[index],
            recv_sem=recv_sem.at[index],
            device_id=above if end else below,
            device_id_type=MESH,
        )

    def push(phase, group, end):
        index = (phase * GROUPS + group) * 2 + end
        block = landing(phase, group).at[end, my_half]
        return pltpu.make_async_remote_copy(
            src_ref=block,
            dst_ref=block,
            send_sem=push_sem.at[index],
            recv_sem=pull_sem.at[index],
            device_id=partner,
            device_id_type=MESH,
        )

    def start(phase, group):
        for end in (0, 1):
            copy = hop(phase, group, end)
            copy.start()
            sends.append(copy)

    def arrive(phase, group):
        for end in (0, 1):
            hop(phase, group, end).wait_recv()
        distance, column = ORDER[phase][group]
        if (distance + 1, column + 1) in ORDER[phase]:
            start(phase, ORDER[phase].index((distance + 1, column + 1)))
        for end in (0, 1):
            copy = push(phase, group, end)
            copy.start()
            sends.append(copy)
        for end in (0, 1):
            push(phase, group, end).wait_recv()

    def term(left, i, distance, column, tile_at):
        at = (panel * rows + i) * (SPREAD * KP)
        first = (distance + HALF) * KP
        wanted = (column + HALF) * KP
        offered = (column - distance + HALF) * KP
        columns = [pat[at + wanted + u] for u in range(KP)]
        deep = []
        for s in range(KP):
            k = pat[at + first + s]
            held = [pat[k * (SPREAD * KP) + offered + t] for t in range(KP)]
            wide = []
            for u in range(KP):
                second = held[1] == columns[u]
                found = jnp.logical_or(held[0] == columns[u], second)
                tile = tile_at(k % rows, jnp.where(second, 1, 0))
                wide.append(jnp.where(found, tile, jnp.zeros_like(tile)))
            deep.append(jnp.concatenate(wide, axis=1))
        weights = jnp.concatenate(deep, axis=0)
        factor = jnp.concatenate([left[i, first], left[i, first + 1]], axis=1)
        return jnp.dot(factor, weights, preferred_element_type=jnp.float32)

    def own_terms(left, right, column):
        def step(n, carry):
            for q in range(UNROLL):
                i = n * UNROLL + q
                acc[column + HALF, i] = term(left, i, 0, column, lambda r, t: right[r, (column + HALF) * KP + t])
            return carry

        lax.fori_loop(0, rows // UNROLL, step, 0)

    def group_terms(left, phase, group):
        distance, column = ORDER[phase][group]
        buffer = landing(phase, group)
        per = rows // UNROLL

        def step(n, carry):
            end = n // per
            sign = 1 - 2 * end
            for q in range(UNROLL):
                i = (n % per) * UNROLL + q
                here = sign * column
                acc[here + HALF, i] += term(left, i, sign * distance, here, lambda r, t: buffer[end, r, t])
            return carry

        lax.fori_loop(0, 2 * per, step, 0)

    def settle(column):
        def step(i, carry):
            total = acc[column + HALF, i]
            for u in range(KP):
                slot = (column + HALF) * KP + u
                tile = total[:, u * side : (u + 1) * side].astype(jnp.bfloat16)
                sv[i, slot] = tile
                mixed = coef[1] * xv[i, slot].astype(jnp.float32) + coef[2] * tile.astype(jnp.float32)
                if slot == HALF * KP:
                    down = lax.broadcasted_iota(jnp.int32, (side, side), 0)
                    across = lax.broadcasted_iota(jnp.int32, (side, side), 1)
                    mixed = mixed + jnp.where(down == across, coef[0], 0.0)
                bv[i, slot] = mixed.astype(jnp.bfloat16)
            return carry

        lax.fori_loop(0, rows, step, 0)
        own_terms(gv, bv, column)
        put(0, column, sv, squared_hbm)

    def put(which, column, source, target):
        slots = pl.ds((column + HALF) * KP, KP)
        copy = pltpu.make_async_copy(source.at[:, slots], target.at[:, slots], out_sem.at[which * SPREAD + column + HALF])
        copy.start()
        outs.append(copy)

    def finish(column):
        def step(i, carry):
            total = acc[column + HALF, i]
            for u in range(KP):
                rv[i, (column + HALF) * KP + u] = total[:, u * side : (u + 1) * side].astype(jnp.bfloat16)
            return carry

        lax.fori_loop(0, rows, step, 0)
        put(1, column, rv, result_hbm)

    outs = []
    loads[0].wait()
    for group in range(NEAR):
        start(0, group)
    for column in range(-HALF, HALF + 1):
        own_terms(xv, xv, column)
    loads[1].wait()
    for group in range(NEAR):
        arrive(0, group)
        group_terms(xv, 0, group)
    arrive(0, 4)
    group_terms(xv, 0, 4)
    settle(2)
    settle(-2)
    start(1, 0)
    arrive(0, 5)
    group_terms(xv, 0, 5)
    settle(1)
    settle(-1)
    start(1, 1)
    start(1, 2)
    arrive(0, 6)
    group_terms(xv, 0, 6)
    settle(0)
    start(1, 3)
    for group in range(NEAR):
        arrive(1, group)
        group_terms(gv, 1, group)
    for group in range(NEAR, GROUPS):
        arrive(1, group)
        group_terms(gv, 1, group)
        column = ORDER[1][group][1]
        finish(column)
        if column:
            finish(-column)
    for copy in outs:
        copy.wait()
    for copy in sends:
        copy.wait_send()


def _unpack(scratch):
    at = 6
    near0, near1 = scratch[at : at + 4], scratch[at + 4 : at + 8]
    far0, far1 = scratch[at + 8 : at + 11], scratch[at + 11 : at + 14]
    return scratch[:6] + (near0, near1, far0, far1) + scratch[at + 14 :]


def solution(mesh):
    panels = mesh.shape["rows"]
    copies = mesh.shape["rep"] // 2

    def local(x_tiles, giant_tiles, coeffs, pattern):
        rows, slots, side, _ = x_tiles.shape
        tiles = pltpu.VMEM(x_tiles.shape, jnp.bfloat16)
        chunk = pltpu.VMEM((2, rows, KP, side, side), jnp.bfloat16)
        moves = 2 * GROUPS * 2
        outs = jax.ShapeDtypeStruct(x_tiles.shape, jnp.bfloat16)
        return pl.pallas_call(
            functools.partial(kernel, panels, 4, copies),
            out_shape=(outs, outs),
            in_specs=[
                pl.BlockSpec(memory_space=pltpu.SMEM),
                pl.BlockSpec(memory_space=pltpu.SMEM),
                pl.BlockSpec(memory_space=pl.ANY),
                pl.BlockSpec(memory_space=pl.ANY),
            ],
            out_specs=(pl.BlockSpec(memory_space=pl.ANY), pl.BlockSpec(memory_space=pl.ANY)),
            scratch_shapes=[
                tiles,
                tiles,
                tiles,
                tiles,
                tiles,
                pltpu.VMEM((SPREAD, rows, side, KP * side), jnp.float32),
                *[chunk for _ in range(2 * GROUPS)],
                pltpu.SemaphoreType.DMA((2,)),
                pltpu.SemaphoreType.DMA((2 * SPREAD,)),
                pltpu.SemaphoreType.DMA((moves,)),
                pltpu.SemaphoreType.DMA((moves,)),
                pltpu.SemaphoreType.DMA((moves,)),
                pltpu.SemaphoreType.DMA((moves,)),
            ],
            compiler_params=pltpu.CompilerParams(
                collective_id=0, has_side_effects=True, vmem_limit_bytes=60 * 1024 * 1024
            ),
        )(pattern.reshape(-1), coeffs, x_tiles, giant_tiles)

    return jax.shard_map(
        local,
        mesh=mesh,
        in_specs=(P("rows", None, None, None), P("rows", None, None, None), P(), P()),
        out_specs=(P("rows", None, None, None), P("rows", None, None, None)),
        check_vma=False,
    )
```

time: 517 us -> 107 us (0.21); the launches traced: 510 us -> 106 us
  waiting for transfers between devices: 288 us -> 0 us
  local copies, waits for them, and re-layouts: 120 us -> 6.88 us
  Pallas kernels: 0 us -> 98.8 us
  matrix products: 73.6 us -> 0 us
  starting transfers between devices: 23.6 us -> 0 us
    ppermute x8 -> x0, waiting for transfers between devices: 288 us -> none  [passed_along(): return lax.ppermute(block, axis, route)]
    pallas_call x0 -> x1, Pallas kernels: none -> 98.8 us  [local(): pl.pallas_call(functools.partial(kernel, panels, 4, copies), out_shape=(o...]
    gather x15 -> x0, local copies, waits for them, and re-layouts: 87.7 us -> none  [the longest x10 84.9 us: panel_terms(): jnp.take(flat_tiles, local_rows[:, :, None] * tile_count + slot_pick, axi...]
    dot_general x10 -> x0, matrix products: 73.6 us -> none  [panel_terms(): jnp.einsum('raxz,rauzy->ruxy', left_part, chosen, preferred_element_type=...]
    ppermute x8 -> x0, starting transfers between devices: 23.6 us -> none  [passed_along(): return lax.ppermute(block, axis, route)]
    reshape x5 -> x1, local copies, waits for them, and re-layouts: 16.3 us -> 0.79 us  [local(): pattern.reshape(-1)]
    unnamed x18 -> x5, local copies, waits for them, and re-layouts: 12.2 us -> 6.1 us
  transfers between devices with their start and end apart: 8 -> 0, of which waited for: 8 -> 0; matrix products, arithmetic and copies ran while one was open for 28% -> 0% of each run, Pallas kernels for 0% -> 0%
where the time goes in v1:
time: 107 us; the launch traced here: 106 us
  Pallas kernels  98.8 us (92%)
  local copies, waits for them, and re-layouts  6.88 us (6%)
    pallas_call x1, Pallas kernels, local(): pl.pallas_call(functools.partial(kernel, panels, 4, copies), out_shape=(o...  98.8 us
    unnamed x5, local copies, waits for them, and re-layouts  6.1 us

profile of v1, /device:TPU:1, one launch (start us, length us, event | category | flops | bytes accessed | tf_op | source)
XLA Modules:
  0.0 106.3 jit_solution(3305306127277704883)
XLA Ops:
  0.6 0.9 copy.6
  1.5 0.8 reshape.7.pat
  2.3 98.8 %shard_map.59 = (bf16[8,10,128,128]{3,2,1,0:T(8,128)(2,1)}, bf16[8,10,128,128]{3,2,1,0:T(8,128)(2,1)}) custom-call(s32[5120]{0:T(1024)} %reshape.7.pat, f32[3]{0:T(128)} %coef.1, bf16[8,10,128,128]{3,2,1,0:T(8,128)(2,1)} %x_hbm.1, bf16[8,10,128,128]{3,2,1,0:T(8,128)(2,1)} %g_hbm.1), custom_call_target="tpu_custom_call" | custom-call | tf_op jit(solution)/shard_map/pallas_call | solution.py:250
  101.1 0.0 copy-start
  101.1 3.7 %copy.9 = bf16[8,10,128,128]{3,2,1,0:T(8,128)(2,1)} copy(bf16[8,10,128,128]{3,2,1,0:T(8,128)(2,1)} %get-tuple-element.4) | data formatting | bytes 5242880
  104.8 0.0 copy-done
  104.8 1.5 %copy.10 = bf16[8,10,128,128]{3,2,1,0:T(8,128)(2,1)} copy(bf16[8,10,128,128]{3,2,1,0:T(8,128)(2,1)S(1)} %copy-done) | data formatting | bytes 5242880
Async XLA Ops:
  101.1 3.7 %copy-start = (bf16[8,10,128,128]{3,2,1,0:T(8,128)(2,1)S(1)}, bf16[8,10,128,128]{3,2,1,0:T(8,128)(2,1)}, u32[]{:S(2)}) copy-start(bf16[8,10,128,128]{3,2,1,0:T(8,128)(2,1)} %get-tuple-element.5) | copy-start | bytes 7864324

commit v2 on v1

v2 whole, which is shorter than its diff:
```python
import functools

import jax
import jax.numpy as jnp
from jax import lax
from jax.experimental import pallas as pl
from jax.experimental.pallas import tpu as pltpu
from jax.sharding import PartitionSpec as P

HALF = 2
KP = 2
SPREAD = 2 * HALF + 1
UNROLL = 4
MESH = pl.DeviceIdType.MESH

ORDER = (
    ((1, -1), (1, 0), (1, 1), (1, 2), (2, 0), (2, 1), (2, 2)),
    ((1, 1), (2, 1), (1, 2), (2, 2)),
)
FORMED = ((1, -1), (1, 0), (2, 0))
MOVES = [(phase, group) for phase in (0, 1) for group in ORDER[phase]]


def kernel(panels, run, copies, pat, coef, x_hbm, g_hbm, squared_hbm, result_hbm, *scratch):
    xv, gv, bv, sv, rv, acc = scratch[:6]
    arrived = dict(zip(MOVES, scratch[6:]))
    formed = dict(zip(FORMED, scratch[6 + len(MOVES) :]))
    load_sem, out_sem, send_sem, recv_sem, push_sem, pull_sem = scratch[-6:]
    rows = xv.shape[0]
    side = xv.shape[2]
    half = rows // 2
    panel = lax.axis_index("rows")
    rep = lax.axis_index("rep")
    core = rep % 2
    zone = rep // 2
    place = panel % run
    if copies > 1:
        zone_up = jnp.where(place == run - 1, 1 - zone, zone)
        zone_down = jnp.where(place == 0, 1 - zone, zone)
    else:
        zone_up = zone
        zone_down = zone
    above = ((panel + 1) % panels, zone_up * 2 + core)
    below = ((panel + panels - 1) % panels, zone_down * 2 + core)
    partner = (panel, zone * 2 + 1 - core)

    loads = [pltpu.make_async_copy(x_hbm, xv, load_sem.at[0]), pltpu.make_async_copy(g_hbm, gv, load_sem.at[1])]
    for load in loads:
        load.start()

    barrier = pltpu.get_barrier_semaphore()
    for other in (above, below, partner):
        pl.semaphore_signal(barrier, inc=1, device_id=other, device_id_type=MESH)
    pl.semaphore_wait(barrier, 3)

    mine = (xv, bv)
    my_half = pl.ds(core * half, half)
    sends = []
    outs = []

    def hop(phase, group, end):
        distance, column = group
        if distance == 1:
            slots = (1 - 2 * end) * (column - distance) + HALF
            source = mine[phase].at[my_half, pl.ds(slots * KP, KP)]
        else:
            passed = (distance - 1, column - 1)
            held = formed[passed] if phase and passed in FORMED else arrived[phase, passed]
            source = held.at[end, my_half]
        index = MOVES.index((phase, group)) * 2 + end
        return pltpu.make_async_remote_copy(
            src_ref=source,
            dst_ref=arrived[phase, group].at[end, my_half],
            send_sem=send_sem.at[index],
            recv_sem=recv_sem.at[index],
            device_id=above if end else below,
            device_id_type=MESH,
        )

    def push(phase, group, end):
        index = MOVES.index((phase, group)) * 2 + end
        block = arrived[phase, group].at[end, my_half]
        return pltpu.make_async_remote_copy(
            src_ref=block,
            dst_ref=block,
            send_sem=push_sem.at[index],
            recv_sem=pull_sem.at[index],
            device_id=partner,
            device_id_type=MESH,
        )

    def start(phase, group):
        for end in (0, 1):
            copy = hop(phase, group, end)
            copy.start()
            sends.append(copy)

    def arrive(phase, group, passing=None):
        for end in (0, 1):
            hop(phase, group, end).wait_recv()
        if passing:
            start(phase, passing)
        for end in (0, 1):
            copy = push(phase, group, end)
            copy.start()
            sends.append(copy)
        for end in (0, 1):
            push(phase, group, end).wait_recv()

    def term(i, row, middle, column, left_at, right_at):
        at = ((panel + row + panels) % panels * rows + i) * (SPREAD * KP)
        first = (middle - row + HALF) * KP
        wanted = (column - row + HALF) * KP
        offered = (column - middle + HALF) * KP
        columns = [pat[at + wanted + u] for u in range(KP)]
        deep = []
        for s in range(KP):
            k = pat[at + first + s]
            held = [pat[k * (SPREAD * KP) + offered + t] for t in range(KP)]
            wide = []
            for u in range(KP):
                second = held[1] == columns[u]
                found = jnp.logical_or(held[0] == columns[u], second)
                tile = right_at(k % rows, jnp.where(second, 1, 0))
                wide.append(jnp.where(found, tile, jnp.zeros_like(tile)))
            deep.append(jnp.concatenate(wide, axis=1))
        weights = jnp.concatenate(deep, axis=0)
        factor = jnp.concatenate([left_at(i, s) for s in range(KP)], axis=1)
        return jnp.dot(factor, weights, preferred_element_type=jnp.float32)

    def tiles_of(ref, offset):
        return lambda i, s: ref[i, (offset + HALF) * KP + s]

    def chunk_of(ref, end):
        return lambda i, s: ref[end, i, s]

    def own_terms(left, right, column):
        def step(n, carry):
            for q in range(UNROLL):
                i = n * UNROLL + q
                acc[column + HALF, i] = term(i, 0, 0, column, tiles_of(left, 0), tiles_of(right, column))
            return carry

        lax.fori_loop(0, rows // UNROLL, step, 0)

    def group_terms(left, buffer, group):
        distance, column = group
        per = rows // UNROLL

        def step(n, carry):
            end = n // per
            sign = 1 - 2 * end
            middle, here = sign * distance, sign * column
            for q in range(UNROLL):
                i = (n % per) * UNROLL + q
                acc[here + HALF, i] += term(i, 0, middle, here, tiles_of(left, middle), chunk_of(buffer, end))
            return carry

        lax.fori_loop(0, 2 * per, step, 0)

    def mix(x_tile, total):
        tile = total.astype(jnp.bfloat16)
        return tile, coef[1] * x_tile.astype(jnp.float32) + coef[2] * tile.astype(jnp.float32)

    def form(group):
        distance, column = group
        per = rows // 2

        def step(n, carry):
            end = n // per
            sign = 1 - 2 * end
            for q in range(2):
                i = (n % per) * 2 + q
                total = None
                for middle in range(distance - HALF, column + HALF + 1):
                    left_at = chunk_of(arrived[0, (distance, middle)], end)
                    if middle > 0:
                        right_at = chunk_of(arrived[0, (middle, column)], end)
                    elif middle < 0:
                        right_at = chunk_of(arrived[0, (-middle, -column)], 1 - end)
                    else:
                        right_at = tiles_of(xv, sign * column)
                    product = term(i, sign * distance, sign * middle, sign * column, left_at, right_at)
                    total = product if total is None else total + product
                for u in range(KP):
                    x_tile = arrived[0, group][end, i, u]
                    formed[group][end, i, u] = mix(x_tile, total[:, u * side : (u + 1) * side])[1].astype(jnp.bfloat16)
            return carry

        lax.fori_loop(0, 2 * per, step, 0)

    def settle(column):
        def step(i, carry):
            total = acc[column + HALF, i]
            for u in range(KP):
                slot = (column + HALF) * KP + u
                tile, mixed = mix(xv[i, slot], total[:, u * side : (u + 1) * side])
                sv[i, slot] = tile
                if slot == HALF * KP:
                    down = lax.broadcasted_iota(jnp.int32, (side, side), 0)
                    across = lax.broadcasted_iota(jnp.int32, (side, side), 1)
                    mixed = mixed + jnp.where(down == across, coef[0], 0.0)
                bv[i, slot] = mixed.astype(jnp.bfloat16)
            return carry

        lax.fori_loop(0, rows, step, 0)
        own_terms(gv, bv, column)
        put(0, column, sv, squared_hbm)

    def put(which, column, source, target):
        slots = pl.ds((column + HALF) * KP, KP)
        copy = pltpu.make_async_copy(source.at[:, slots], target.at[:, slots], out_sem.at[which * SPREAD + column + HALF])
        copy.start()
        outs.append(copy)

    def finish(column):
        def step(i, carry):
            total = acc[column + HALF, i]
            for u in range(KP):
                rv[i, (column + HALF) * KP + u] = total[:, u * side : (u + 1) * side].astype(jnp.bfloat16)
            return carry

        lax.fori_loop(0, rows, step, 0)
        put(1, column, rv, result_hbm)

    loads[0].wait()
    for group in ORDER[0][:4]:
        start(0, group)
    for column in range(-HALF, HALF + 1):
        own_terms(xv, xv, column)
    loads[1].wait()
    for group in ORDER[0][:4]:
        onward = (group[0] + 1, group[1] + 1)
        arrive(0, group, onward if onward in ORDER[0] else None)
        group_terms(xv, arrived[0, group], group)
    form((1, -1))
    arrive(0, (2, 0))
    group_terms(xv, arrived[0, (2, 0)], (2, 0))
    settle(0)
    start(1, (1, 1))
    form((1, 0))
    start(1, (2, 1))
    arrive(0, (2, 1))
    group_terms(xv, arrived[0, (2, 1)], (2, 1))
    settle(1)
    settle(-1)
    start(1, (1, 2))
    arrive(0, (2, 2))
    group_terms(xv, arrived[0, (2, 2)], (2, 2))
    settle(2)
    settle(-2)
    form((2, 0))
    arrive(1, (1, 1), (2, 2))
    for group in FORMED:
        group_terms(gv, formed[group], group)
    finish(0)
    group_terms(gv, arrived[1, (1, 1)], (1, 1))
    arrive(1, (2, 1))
    group_terms(gv, arrived[1, (2, 1)], (2, 1))
    finish(1)
    finish(-1)
    arrive(1, (1, 2))
    group_terms(gv, arrived[1, (1, 2)], (1, 2))
    arrive(1, (2, 2))
    group_terms(gv, arrived[1, (2, 2)], (2, 2))
    finish(2)
    finish(-2)
    for copy in outs:
        copy.wait()
    for copy in sends:
        copy.wait_send()


def solution(mesh):
    panels = mesh.shape["rows"]
    copies = mesh.shape["rep"] // 2

    def local(x_tiles, giant_tiles, coeffs, pattern):
        rows, slots, side, _ = x_tiles.shape
        tiles = pltpu.VMEM(x_tiles.shape, jnp.bfloat16)
        chunk = pltpu.VMEM((2, rows, KP, side, side), jnp.bfloat16)
        moves = 2 * len(MOVES)
        outs = jax.ShapeDtypeStruct(x_tiles.shape, jnp.bfloat16)
        return pl.pallas_call(
            functools.partial(kernel, panels, 4, copies),
            out_shape=(outs, outs),
            in_specs=[
                pl.BlockSpec(memory_space=pltpu.SMEM),
                pl.BlockSpec(memory_space=pltpu.SMEM),
                pl.BlockSpec(memory_space=pl.ANY),
                pl.BlockSpec(memory_space=pl.ANY),
            ],
            out_specs=(pl.BlockSpec(memory_space=pl.ANY), pl.BlockSpec(memory_space=pl.ANY)),
            scratch_shapes=[
                tiles,
                tiles,
                tiles,
                tiles,
                tiles,
                pltpu.VMEM((SPREAD, rows, side, KP * side), jnp.float32),
                *[chunk for _ in MOVES + list(FORMED)],
                pltpu.SemaphoreType.DMA((2,)),
                pltpu.SemaphoreType.DMA((2 * SPREAD,)),
                pltpu.SemaphoreType.DMA((moves,)),
                pltpu.SemaphoreType.DMA((moves,)),
                pltpu.SemaphoreType.DMA((moves,)),
                pltpu.SemaphoreType.DMA((moves,)),
            ],
            compiler_params=pltpu.CompilerParams(
                collective_id=0, has_side_effects=True, vmem_limit_bytes=60 * 1024 * 1024
            ),
        )(pattern.reshape(-1), coeffs, x_tiles, giant_tiles)

    return jax.shard_map(
        local,
        mesh=mesh,
        in_specs=(P("rows", None, None, None), P("rows", None, None, None), P(), P()),
        out_specs=(P("rows", None, None, None), P("rows", None, None, None)),
        check_vma=False,
    )
```

time: 107 us -> 89.9 us (0.84)
  Pallas kernels: 98.8 us -> 82.1 us
    pallas_call x1, Pallas kernels: 98.8 us -> 82.1 us  [local(): pl.pallas_call(functools.partial(kernel, panels, 4, copies), out_shape=(o...]
where the time goes in v2:
time: 89.9 us; the launch traced here: 89.7 us
  Pallas kernels  82.1 us (91%)
  local copies, waits for them, and re-layouts  6.88 us (8%)
    pallas_call x1, Pallas kernels, local(): pl.pallas_call(functools.partial(kernel, panels, 4, copies), out_shape=(o...  82.1 us
    unnamed x5, local copies, waits for them, and re-layouts  6.1 us

profile of v2, /device:TPU:1, one launch (start us, length us, event | category | flops | bytes accessed | tf_op | source)
XLA Modules:
  0.0 89.7 jit_solution(11629817055029449749)
XLA Ops:
  0.6 0.9 copy.6
  1.5 0.8 reshape.7.pat
  2.3 82.1 %shard_map.59 = (bf16[8,10,128,128]{3,2,1,0:T(8,128)(2,1)}, bf16[8,10,128,128]{3,2,1,0:T(8,128)(2,1)}) custom-call(s32[5120]{0:T(1024)} %reshape.7.pat, f32[3]{0:T(128)} %coef.1, bf16[8,10,128,128]{3,2,1,0:T(8,128)(2,1)} %x_hbm.1, bf16[8,10,128,128]{3,2,1,0:T(8,128)(2,1)} %g_hbm.1), custom_call_target="tpu_custom_call" | custom-call | tf_op jit(solution)/shard_map/pallas_call | solution.py:284
  84.4 0.0 copy-start
  84.4 3.7 %copy.9 = bf16[8,10,128,128]{3,2,1,0:T(8,128)(2,1)} copy(bf16[8,10,128,128]{3,2,1,0:T(8,128)(2,1)} %get-tuple-element.4) | data formatting | bytes 5242880
  88.2 0.0 copy-done
  88.2 1.5 %copy.10 = bf16[8,10,128,128]{3,2,1,0:T(8,128)(2,1)} copy(bf16[8,10,128,128]{3,2,1,0:T(8,128)(2,1)S(1)} %copy-done) | data formatting | bytes 5242880
Async XLA Ops:
  84.4 3.7 %copy-start = (bf16[8,10,128,128]{3,2,1,0:T(8,128)(2,1)S(1)}, bf16[8,10,128,128]{3,2,1,0:T(8,128)(2,1)}, u32[]{:S(2)}) copy-start(bf16[8,10,128,128]{3,2,1,0:T(8,128)(2,1)} %get-tuple-element.5) | copy-start | bytes 7864324

commit v3 on v2

--- a/solution.py
+++ b/solution.py
@@ -19,13 +19,14 @@
 )
 FORMED = ((1, -1), (1, 0), (2, 0))
 MOVES = [(phase, group) for phase in (0, 1) for group in ORDER[phase]]
-
-
-def kernel(panels, run, copies, pat, coef, x_hbm, g_hbm, squared_hbm, result_hbm, *scratch):
-    xv, gv, bv, sv, rv, acc = scratch[:6]
-    arrived = dict(zip(MOVES, scratch[6:]))
-    formed = dict(zip(FORMED, scratch[6 + len(MOVES) :]))
-    load_sem, out_sem, send_sem, recv_sem, push_sem, pull_sem = scratch[-6:]
+SHARED = MOVES + [("formed", group) for group in FORMED]
+
+
+def kernel(panels, run, copies, pat, coef, x_hbm, g_hbm, sv, rv, *scratch):
+    xv, gv, bv, acc = scratch[:4]
+    arrived = dict(zip(SHARED, scratch[4:]))
+    formed = {group: arrived["formed", group] for group in FORMED}
+    load_sem, send_sem, recv_sem, push_sem, pull_sem = scratch[-5:]
     rows = xv.shape[0]
     side = xv.shape[2]
     half = rows // 2
@@ -56,7 +57,6 @@
     mine = (xv, bv)
     my_half = pl.ds(core * half, half)
     sends = []
-    outs = []
 
     def hop(phase, group, end):
         distance, column = group
@@ -77,9 +77,9 @@
             device_id_type=MESH,
         )
 
-    def push(phase, group, end):
-        index = MOVES.index((phase, group)) * 2 + end
-        block = arrived[phase, group].at[end, my_half]
+    def push(key, end):
+        index = SHARED.index(key) * 2 + end
+        block = arrived[key].at[end, my_half]
         return pltpu.make_async_remote_copy(
             src_ref=block,
             dst_ref=block,
@@ -95,28 +95,34 @@
             copy.start()
             sends.append(copy)
 
-    def arrive(phase, group, passing=None):
+    def share(key):
+        for end in (0, 1):
+            copy = push(key, end)
+            copy.start()
+            sends.append(copy)
+
+    def arrive(phase, group):
         for end in (0, 1):
             hop(phase, group, end).wait_recv()
-        if passing:
-            start(phase, passing)
+        onward = (group[0] + 1, group[1] + 1)
+        if onward in ORDER[phase] and not (phase and group in FORMED):
+            start(phase, onward)
+        share((phase, group))
+
+    def whole(key):
         for end in (0, 1):
-            copy = push(phase, group, end)
-            copy.start()
-            sends.append(copy)
-        for end in (0, 1):
-            push(phase, group, end).wait_recv()
+            push(key, end).wait_recv()
 
     def term(i, row, middle, column, left_at, right_at):
-        at = ((panel + row + panels) % panels * rows + i) * (SPREAD * KP)
+        at = (panel + row + panels) % panels * rows + i
         first = (middle - row + HALF) * KP
         wanted = (column - row + HALF) * KP
         offered = (column - middle + HALF) * KP
-        columns = [pat[at + wanted + u] for u in range(KP)]
+        columns = [pat[wanted + u, at] for u in range(KP)]
         deep = []
         for s in range(KP):
-            k = pat[at + first + s]
-            held = [pat[k * (SPREAD * KP) + offered + t] for t in range(KP)]
+            k = pat[first + s, at]
+            held = [pat[offered + t, k] for t in range(KP)]
             wide = []
             for u in range(KP):
                 second = held[1] == columns[u]
@@ -164,13 +170,13 @@
 
     def form(group):
         distance, column = group
-        per = rows // 2
+        per = half // 2
 
         def step(n, carry):
             end = n // per
             sign = 1 - 2 * end
             for q in range(2):
-                i = (n % per) * 2 + q
+                i = core * half + (n % per) * 2 + q
                 total = None
                 for middle in range(distance - HALF, column + HALF + 1):
                     left_at = chunk_of(arrived[0, (distance, middle)], end)
@@ -188,6 +194,7 @@
             return carry
 
         lax.fori_loop(0, 2 * per, step, 0)
+        share(("formed", group))
 
     def settle(column):
         def step(i, carry):
@@ -205,13 +212,6 @@
 
         lax.fori_loop(0, rows, step, 0)
         own_terms(gv, bv, column)
-        put(0, column, sv, squared_hbm)
-
-    def put(which, column, source, target):
-        slots = pl.ds((column + HALF) * KP, KP)
-        copy = pltpu.make_async_copy(source.at[:, slots], target.at[:, slots], out_sem.at[which * SPREAD + column + HALF])
-        copy.start()
-        outs.append(copy)
 
     def finish(column):
         def step(i, carry):
@@ -221,7 +221,15 @@
             return carry
 
         lax.fori_loop(0, rows, step, 0)
-        put(1, column, rv, result_hbm)
+
+    def add_x(group):
+        whole((0, group))
+        group_terms(xv, arrived[0, group], group)
+
+    def add_baby(group):
+        key = ("formed" if group in FORMED else 1, group)
+        whole(key)
+        group_terms(gv, arrived[key], group)
 
     loads[0].wait()
     for group in ORDER[0][:4]:
@@ -229,46 +237,54 @@
     for column in range(-HALF, HALF + 1):
         own_terms(xv, xv, column)
     loads[1].wait()
-    for group in ORDER[0][:4]:
-        onward = (group[0] + 1, group[1] + 1)
-        arrive(0, group, onward if onward in ORDER[0] else None)
-        group_terms(xv, arrived[0, group], group)
+    for group in ORDER[0][:3]:
+        arrive(0, group)
+        add_x(group)
     form((1, -1))
+    arrive(0, (1, 2))
+    add_x((1, 2))
     arrive(0, (2, 0))
-    group_terms(xv, arrived[0, (2, 0)], (2, 0))
+    add_x((2, 0))
     settle(0)
     start(1, (1, 1))
     form((1, 0))
     start(1, (2, 1))
     arrive(0, (2, 1))
-    group_terms(xv, arrived[0, (2, 1)], (2, 1))
+    add_x((2, 1))
     settle(1)
     settle(-1)
     start(1, (1, 2))
     arrive(0, (2, 2))
-    group_terms(xv, arrived[0, (2, 2)], (2, 2))
+    form((2, 0))
+    add_x((2, 2))
     settle(2)
     settle(-2)
-    form((2, 0))
-    arrive(1, (1, 1), (2, 2))
-    for group in FORMED:
-        group_terms(gv, formed[group], group)
+    add_baby((1, -1))
+    arrive(1, (1, 1))
+    add_baby((1, 0))
+    add_baby((2, 0))
     finish(0)
-    group_terms(gv, arrived[1, (1, 1)], (1, 1))
+    add_baby((1, 1))
     arrive(1, (2, 1))
-    group_terms(gv, arrived[1, (2, 1)], (2, 1))
+    add_baby((2, 1))
     finish(1)
     finish(-1)
     arrive(1, (1, 2))
-    group_terms(gv, arrived[1, (1, 2)], (1, 2))
+    add_baby((1, 2))
     arrive(1, (2, 2))
-    group_terms(gv, arrived[1, (2, 2)], (2, 2))
+    add_baby((2, 2))
     finish(2)
     finish(-2)
-    for copy in outs:
-        copy.wait()
     for copy in sends:
         copy.wait_send()
+
+
+def write(squared, result, squared_hbm, result_hbm, sem):
+    copies = [pltpu.make_async_copy(squared, squared_hbm, sem.at[0]), pltpu.make_async_copy(result, result_hbm, sem.at[1])]
+    for copy in copies:
+        copy.start()
+    for copy in copies:
+        copy.wait()
 
 
 def solution(mesh):
@@ -279,37 +295,41 @@
         rows, slots, side, _ = x_tiles.shape
         tiles = pltpu.VMEM(x_tiles.shape, jnp.bfloat16)
         chunk = pltpu.VMEM((2, rows, KP, side, side), jnp.bfloat16)
-        moves = 2 * len(MOVES)
         outs = jax.ShapeDtypeStruct(x_tiles.shape, jnp.bfloat16)
-        return pl.pallas_call(
+        held = pl.pallas_call(
             functools.partial(kernel, panels, 4, copies),
             out_shape=(outs, outs),
             in_specs=[
                 pl.BlockSpec(memory_space=pltpu.SMEM),
                 pl.BlockSpec(memory_space=pltpu.SMEM),
-                pl.BlockSpec(memory_space=pl.ANY),
-                pl.BlockSpec(memory_space=pl.ANY),
+                pl.BlockSpec(memory_space=pltpu.HBM),
+                pl.BlockSpec(memory_space=pltpu.HBM),
             ],
-            out_specs=(pl.BlockSpec(memory_space=pl.ANY), pl.BlockSpec(memory_space=pl.ANY)),
+            out_specs=(pl.BlockSpec(memory_space=pltpu.VMEM), pl.BlockSpec(memory_space=pltpu.VMEM)),
             scratch_shapes=[
                 tiles,
                 tiles,
                 tiles,
-                tiles,
-                tiles,
                 pltpu.VMEM((SPREAD, rows, side, KP * side), jnp.float32),
-                *[chunk for _ in MOVES + list(FORMED)],
+                *[chunk for _ in SHARED],
                 pltpu.SemaphoreType.DMA((2,)),
-                pltpu.SemaphoreType.DMA((2 * SPREAD,)),
-                pltpu.SemaphoreType.DMA((moves,)),
-                pltpu.SemaphoreType.DMA((moves,)),
-                pltpu.SemaphoreType.DMA((moves,)),
-                pltpu.SemaphoreType.DMA((moves,)),
+                pltpu.SemaphoreType.DMA((2 * len(MOVES),)),
+                pltpu.SemaphoreType.DMA((2 * len(MOVES),)),
+                pltpu.SemaphoreType.DMA((2 * len(SHARED),)),
+                pltpu.SemaphoreType.DMA((2 * len(SHARED),)),
             ],
             compiler_params=pltpu.CompilerParams(
-                collective_id=0, has_side_effects=True, vmem_limit_bytes=60 * 1024 * 1024
+                collective_id=0, has_side_effects=True, vmem_limit_bytes=47 * 1024 * 1024
             ),
-        )(pattern.reshape(-1), coeffs, x_tiles, giant_tiles)
+        )(pattern.T, coeffs, x_tiles, giant_tiles)
+        return pl.pallas_call(
+            write,
+            out_shape=(outs, outs),
+            in_specs=[pl.BlockSpec(memory_space=pltpu.VMEM)] * 2,
+            out_specs=(pl.BlockSpec(memory_space=pltpu.HBM), pl.BlockSpec(memory_space=pltpu.HBM)),
+            scratch_shapes=[pltpu.SemaphoreType.DMA((2,))],
+            compiler_params=pltpu.CompilerParams(vmem_limit_bytes=8 * 1024 * 1024),
+        )(*held)
 
     return jax.shard_map(
         local,

time: 89.9 us -> 85.3 us (0.949)
  local copies, waits for them, and re-layouts: 6.88 us -> 1.41 us
  Pallas kernels: 82.1 us -> 83.1 us
    unnamed x5 -> x4, local copies, waits for them, and re-layouts: 6.1 us -> 1.41 us
    pallas_call x0 -> x1, Pallas kernels: none -> 2.37 us  [local(): pl.pallas_call(write, out_shape=(outs, outs), in_specs=[pl.BlockSpec(memo...]
    pallas_call x1, Pallas kernels: 82.1 us -> 80.7 us  [local(): pl.pallas_call(functools.partial(kernel, panels, 4, copies), out_shape=(o...]
where the time goes in v3:
time: 85.3 us; the launch traced here: 85.2 us
  Pallas kernels  83.1 us (97%)
  local copies, waits for them, and re-layouts  1.41 us (2%)
    pallas_call x1, Pallas kernels, local(): pl.pallas_call(functools.partial(kernel, panels, 4, copies), out_shape=(o...  80.7 us
    pallas_call x1, Pallas kernels, local(): pl.pallas_call(write, out_shape=(outs, outs), in_specs=[pl.BlockSpec(memo...  2.37 us

profile of v3, /device:TPU:1, one launch (start us, length us, event | category | flops | bytes accessed | tf_op | source)
XLA Modules:
  0.0 85.2 jit_solution(5794879673644017500)
XLA Ops:
  0.6 0.0 copy-start
  0.6 0.7 copy-done
  1.4 0.0 copy-start.1
  1.4 0.7 copy-done.1
  2.0 80.7 %shard_map.59 = (bf16[8,10,128,128]{3,2,1,0:T(8,128)(2,1)S(1)}, bf16[8,10,128,128]{3,2,1,0:T(8,128)(2,1)S(1)}) custom-call(s32[10,512]{1,0:T(8,128)S(1)} %bitcast.1, f32[3]{0:T(128)S(1)} %copy-done.1, bf16[8,10,128,128]{3,2,1,0:T(8,128)(2,1)} %x_hbm.1, bf16[8,10,128,128]{3,2,1,0:T(8,128)(2,1)} %g_hbm.1), custom_call_target="tpu_custom_call" | custom-call | tf_op jit(solution)/shard_map/pallas_call | solution.py:299
  82.8 2.4 %shard_map.60 = (bf16[8,10,128,128]{3,2,1,0:T(8,128)(2,1)}, bf16[8,10,128,128]{3,2,1,0:T(8,128)(2,1)}) custom-call(bf16[8,10,128,128]{3,2,1,0:T(8,128)(2,1)S(1)} %get-tuple-element.4.squared, bf16[8,10,128,128]{3,2,1,0:T(8,128)(2,1)S(1)} %get-tuple-element.5.result), custom_call_target="tpu_custom_call" | custom-call | tf_op jit(solution)/shard_map/pallas_call | solution.py:325
Async XLA Ops:
  0.6 0.8 copy-start
  1.4 0.7 copy-start.1

commit v4 on v3

--- a/solution.py
+++ b/solution.py
@@ -10,7 +10,7 @@
 HALF = 2
 KP = 2
 SPREAD = 2 * HALF + 1
-UNROLL = 4
+UNROLL = 8
 MESH = pl.DeviceIdType.MESH
 
 ORDER = (
@@ -22,7 +22,7 @@
 SHARED = MOVES + [("formed", group) for group in FORMED]
 
 
-def kernel(panels, run, copies, pat, coef, x_hbm, g_hbm, sv, rv, *scratch):
+def kernel(panels, run, copies, pat_hbm, coef_hbm, x_hbm, g_hbm, sv, rv, pat, coef, *scratch):
     xv, gv, bv, acc = scratch[:4]
     arrived = dict(zip(SHARED, scratch[4:]))
     formed = {group: arrived["formed", group] for group in FORMED}
@@ -45,16 +45,16 @@
     below = ((panel + panels - 1) % panels, zone_down * 2 + core)
     partner = (panel, zone * 2 + 1 - core)
 
-    loads = [pltpu.make_async_copy(x_hbm, xv, load_sem.at[0]), pltpu.make_async_copy(g_hbm, gv, load_sem.at[1])]
-    for load in loads:
-        load.start()
-
     barrier = pltpu.get_barrier_semaphore()
     for other in (above, below, partner):
         pl.semaphore_signal(barrier, inc=1, device_id=other, device_id_type=MESH)
+    pairs = ((pat_hbm, pat), (coef_hbm, coef), (x_hbm, xv), (g_hbm, gv))
+    loads = [pltpu.make_async_copy(source, target, load_sem.at[n]) for n, (source, target) in enumerate(pairs)]
+    for load in loads:
+        load.start()
     pl.semaphore_wait(barrier, 3)
 
-    mine = (xv, bv)
+    mine = (x_hbm, bv)
     my_half = pl.ds(core * half, half)
     sends = []
 
@@ -149,7 +149,7 @@
 
         lax.fori_loop(0, rows // UNROLL, step, 0)
 
-    def group_terms(left, buffer, group):
+    def group_terms(left, buffer, group, last=False):
         distance, column = group
         per = rows // UNROLL
 
@@ -159,7 +159,12 @@
             middle, here = sign * distance, sign * column
             for q in range(UNROLL):
                 i = (n % per) * UNROLL + q
-                acc[here + HALF, i] += term(i, 0, middle, here, tiles_of(left, middle), chunk_of(buffer, end))
+                total = acc[here + HALF, i] + term(i, 0, middle, here, tiles_of(left, middle), chunk_of(buffer, end))
+                if last:
+                    for u in range(KP):
+                        rv[i, (here + HALF) * KP + u] = total[:, u * side : (u + 1) * side].astype(jnp.bfloat16)
+                else:
+                    acc[here + HALF, i] = total
             return carry
 
         lax.fori_loop(0, 2 * per, step, 0)
@@ -226,17 +231,17 @@
         whole((0, group))
         group_terms(xv, arrived[0, group], group)
 
-    def add_baby(group):
+    def add_baby(group, last=False):
         key = ("formed" if group in FORMED else 1, group)
         whole(key)
-        group_terms(gv, arrived[key], group)
-
-    loads[0].wait()
+        group_terms(gv, arrived[key], group, last)
+
     for group in ORDER[0][:4]:
         start(0, group)
+    for load in loads:
+        load.wait()
     for column in range(-HALF, HALF + 1):
         own_terms(xv, xv, column)
-    loads[1].wait()
     for group in ORDER[0][:3]:
         arrive(0, group)
         add_x(group)
@@ -262,19 +267,15 @@
     add_baby((1, -1))
     arrive(1, (1, 1))
     add_baby((1, 0))
+    add_baby((1, 1))
     add_baby((2, 0))
     finish(0)
-    add_baby((1, 1))
     arrive(1, (2, 1))
-    add_baby((2, 1))
-    finish(1)
-    finish(-1)
+    add_baby((2, 1), last=True)
     arrive(1, (1, 2))
     add_baby((1, 2))
     arrive(1, (2, 2))
-    add_baby((2, 2))
-    finish(2)
-    finish(-2)
+    add_baby((2, 2), last=True)
     for copy in sends:
         copy.wait_send()
 
@@ -300,19 +301,21 @@
             functools.partial(kernel, panels, 4, copies),
             out_shape=(outs, outs),
             in_specs=[
-                pl.BlockSpec(memory_space=pltpu.SMEM),
-                pl.BlockSpec(memory_space=pltpu.SMEM),
+                pl.BlockSpec(memory_space=pltpu.HBM),
+                pl.BlockSpec(memory_space=pltpu.HBM),
                 pl.BlockSpec(memory_space=pltpu.HBM),
                 pl.BlockSpec(memory_space=pltpu.HBM),
             ],
             out_specs=(pl.BlockSpec(memory_space=pltpu.VMEM), pl.BlockSpec(memory_space=pltpu.VMEM)),
             scratch_shapes=[
+                pltpu.SMEM((slots, pattern.shape[0]), jnp.int32),
+                pltpu.SMEM(coeffs.shape, jnp.float32),
                 tiles,
                 tiles,
                 tiles,
                 pltpu.VMEM((SPREAD, rows, side, KP * side), jnp.float32),
                 *[chunk for _ in SHARED],
-                pltpu.SemaphoreType.DMA((2,)),
+                pltpu.SemaphoreType.DMA((4,)),
                 pltpu.SemaphoreType.DMA((2 * len(MOVES),)),
                 pltpu.SemaphoreType.DMA((2 * len(MOVES),)),
                 pltpu.SemaphoreType.DMA((2 * len(SHARED),)),
@@ -321,7 +324,7 @@
             compiler_params=pltpu.CompilerParams(
                 collective_id=0, has_side_effects=True, vmem_limit_bytes=47 * 1024 * 1024
             ),
-        )(pattern.T, coeffs, x_tiles, giant_tiles)
+        )(*(pltpu.with_memory_space_constraint(value, pltpu.HBM) for value in (pattern.T, coeffs, x_tiles, giant_tiles)))
         return pl.pallas_call(
             write,
             out_shape=(outs, outs),

time: 85.3 us -> 81.2 us (0.952)
  Pallas kernels: 83.1 us -> 80.5 us
  local copies, waits for them, and re-layouts: 1.41 us -> 0 us
    pallas_call x1, Pallas kernels: 80.7 us -> 78.1 us  [local(): pl.pallas_call(functools.partial(kernel, panels, 4, copies), out_shape=(o...]
    unnamed x4 -> x0, local copies, waits for them, and re-layouts: 1.41 us -> none
where the time goes in v4:
time: 81.2 us; the launch traced here: 81.1 us
  Pallas kernels  80.5 us (99%)
    pallas_call x1, Pallas kernels, local(): pl.pallas_call(functools.partial(kernel, panels, 4, copies), out_shape=(o...  78.1 us
    pallas_call x1, Pallas kernels, local(): pl.pallas_call(write, out_shape=(outs, outs), in_specs=[pl.BlockSpec(memo...  2.37 us

profile of v4, /device:TPU:1, one launch (start us, length us, event | category | flops | bytes accessed | tf_op | source)
XLA Modules:
  0.0 81.1 jit_solution(14621004227565336421)
XLA Ops:
  0.6 78.1 %shard_map.59 = (bf16[8,10,128,128]{3,2,1,0:T(8,128)(2,1)S(1)}, bf16[8,10,128,128]{3,2,1,0:T(8,128)(2,1)S(1)}) custom-call(s32[10,512]{1,0:T(8,128)} %bitcast.1, f32[3]{0:T(128)} %coef_hbm.1, bf16[8,10,128,128]{3,2,1,0:T(8,128)(2,1)} %x_hbm.1, bf16[8,10,128,128]{3,2,1,0:T(8,128)(2,1)} %g_hbm.1), custom_call_target="tpu_custom_call" | custom-call | tf_op jit(solution)/shard_map/pallas_call | solution.py:300
  78.7 2.4 %shard_map.60 = (bf16[8,10,128,128]{3,2,1,0:T(8,128)(2,1)}, bf16[8,10,128,128]{3,2,1,0:T(8,128)(2,1)}) custom-call(bf16[8,10,128,128]{3,2,1,0:T(8,128)(2,1)S(1)} %get-tuple-element.4.squared, bf16[8,10,128,128]{3,2,1,0:T(8,128)(2,1)S(1)} %get-tuple-element.5.result), custom_call_target="tpu_custom_call" | custom-call | tf_op jit(solution)/shard_map/pallas_call | solution.py:328

commit v5 on v4

--- a/solution.py
+++ b/solution.py
@@ -50,8 +50,6 @@
         pl.semaphore_signal(barrier, inc=1, device_id=other, device_id_type=MESH)
     pairs = ((pat_hbm, pat), (coef_hbm, coef), (x_hbm, xv), (g_hbm, gv))
     loads = [pltpu.make_async_copy(source, target, load_sem.at[n]) for n, (source, target) in enumerate(pairs)]
-    for load in loads:
-        load.start()
     pl.semaphore_wait(barrier, 3)
 
     mine = (x_hbm, bv)
@@ -89,25 +87,25 @@
             device_id_type=MESH,
         )
 
+    def go(copy):
+        copy.start()
+        sends.append(copy)
+
     def start(phase, group):
         for end in (0, 1):
-            copy = hop(phase, group, end)
-            copy.start()
-            sends.append(copy)
+            go(hop(phase, group, end))
 
     def share(key):
         for end in (0, 1):
-            copy = push(key, end)
-            copy.start()
-            sends.append(copy)
+            go(push(key, end))
 
     def arrive(phase, group):
+        onward = (group[0] + 1, group[1] + 1)
         for end in (0, 1):
             hop(phase, group, end).wait_recv()
-        onward = (group[0] + 1, group[1] + 1)
-        if onward in ORDER[phase] and not (phase and group in FORMED):
-            start(phase, onward)
-        share((phase, group))
+            if onward in ORDER[phase] and not (phase and group in FORMED):
+                go(hop(phase, onward, end))
+            go(push((phase, group), end))
 
     def whole(key):
         for end in (0, 1):
@@ -238,6 +236,8 @@
 
     for group in ORDER[0][:4]:
         start(0, group)
+    for load in loads:
+        load.start()
     for load in loads:
         load.wait()
     for column in range(-HALF, HALF + 1):

time: 81.2 us -> 80.8 us (level)
  no operation moved by 1% of the time
where the time goes in v5:
time: 80.8 us; the launch traced here: 80.7 us
  Pallas kernels  80.1 us (99%)
    pallas_call x1, Pallas kernels, local(): pl.pallas_call(functools.partial(kernel, panels, 4, copies), out_shape=(o...  77.7 us
    pallas_call x1, Pallas kernels, local(): pl.pallas_call(write, out_shape=(outs, outs), in_specs=[pl.BlockSpec(memo...  2.37 us

profile of v5, /device:TPU:1, one launch (start us, length us, event | category | flops | bytes accessed | tf_op | source)
XLA Modules:
  0.0 80.7 jit_solution(7021563367460441519)
XLA Ops:
  0.6 77.7 %shard_map.59 = (bf16[8,10,128,128]{3,2,1,0:T(8,128)(2,1)S(1)}, bf16[8,10,128,128]{3,2,1,0:T(8,128)(2,1)S(1)}) custom-call(s32[10,512]{1,0:T(8,128)} %bitcast.1, f32[3]{0:T(128)} %coef_hbm.1, bf16[8,10,128,128]{3,2,1,0:T(8,128)(2,1)} %x_hbm.1, bf16[8,10,128,128]{3,2,1,0:T(8,128)(2,1)} %g_hbm.1), custom_call_target="tpu_custom_call" | custom-call | tf_op jit(solution)/shard_map/pallas_call | solution.py:300
  78.4 2.4 %shard_map.60 = (bf16[8,10,128,128]{3,2,1,0:T(8,128)(2,1)}, bf16[8,10,128,128]{3,2,1,0:T(8,128)(2,1)}) custom-call(bf16[8,10,128,128]{3,2,1,0:T(8,128)(2,1)S(1)} %get-tuple-element.4.squared, bf16[8,10,128,128]{3,2,1,0:T(8,128)(2,1)S(1)} %get-tuple-element.5.result), custom_call_target="tpu_custom_call" | custom-call | tf_op jit(solution)/shard_map/pallas_call | solution.py:328
